TPU v7x, 32 devices: a whole 2x2x4 slice. The times are simulated.
32 devices in a mesh: clip: 2 (over y), outer: 4 (over z), inner: 2 (over x), head: 2 (over core).
Axes of the slice: x: 2, y: 2, z: 4, core: 2. Of those that a mesh axis runs over, the one named last changes fastest.
Arguments:
- tokens: bfloat16 [2, 4096, 3072], P('clip', ('outer', 'inner', 'head')), parts along dimension 0, may hold values from -6 to 6
- shift_mod: float32 [2, 3072], P('clip'), parts along dimension 0, may hold values from -3 to 3
- scale_mod: float32 [2, 3072], P('clip'), parts along dimension 0, may hold values from -1.5 to 1.5
- gate_mod: float32 [2, 3072], P('clip'), parts along dimension 0, may hold values from 0.5 to 2
- query_weight: bfloat16 [3072, 3072], P('outer', ('inner', 'head')), may hold values from -0.109375 to 0.109375
- key_weight: bfloat16 [3072, 3072], P('outer', ('inner', 'head')), may hold values from -0.109375 to 0.109375
- value_weight: bfloat16 [3072, 3072], P('outer', ('inner', 'head')), may hold values from -0.109375 to 0.109375
- out_weight: bfloat16 [3072, 3072], P(('inner', 'head'), 'outer'), may hold values from -0.109375 to 0.109375
- query_gain: float32 [128], replicated, may hold values from 1 to 18, as said below
- key_gain: float32 [128], replicated, may hold values from 1 to 18, as said below
Outputs:
- attended: bfloat16 [2, 4096, 3072], P('clip', ('outer', 'inner', 'head')), parts along dimension 0
There are 2 independent parts, one for each index of `clip`. A program takes and returns all parts, laid end to end along the dimension named above; an argument that names none is the same for every part. Nothing has to cross between parts.
Inputs may be any that keep to these rules, and one draw needn't show every extreme that they name: `query_gain`: 128 positive scales. `key_gain`: 128 positive scales.
All inputs are finite; a program needn't handle non-finite values.
Results may differ from a plain program's by a relative error of at most 0.015.
The roundings to bfloat16 on the way count: a program that leaves them out, or rounds other values in their place, can miss the bound.
Values may be sent and summed in bfloat16 or wider, within the bound.
A program may use at most 192 MiB of HBM per device.

v0:
```python
import math
import jax
import jax.numpy as jnp
from jax import lax
from jax.sharding import PartitionSpec as P

EPSILON = 1e-06


def modulate(tokens, shift_mod, scale_mod):
    values = tokens.astype(jnp.float32)
    center = jnp.mean(values, axis=-1, keepdims=True)
    spread = jnp.mean(jnp.square(values - center), axis=-1, keepdims=True)
    normed = (values - center) / jnp.sqrt(spread + EPSILON)
    return (normed * (1.0 + scale_mod[:, None, :]) + shift_mod[:, None, :]).astype(jnp.bfloat16)


def head_norm(projected, gain_vec, head_dim):
    shaped = projected.reshape(projected.shape[:-1] + (projected.shape[-1] // head_dim, head_dim))
    mean_square = jnp.mean(jnp.square(shaped), axis=-1, keepdims=True)
    return (shaped / jnp.sqrt(mean_square + EPSILON) * gain_vec).astype(jnp.bfloat16)


def per_device(
    tokens,
    shift_mod,
    scale_mod,
    gate_mod,
    query_weight,
    key_weight,
    value_weight,
    out_weight,
    query_gain,
    key_gain,
):
    head_dim = query_gain.shape[0]
    modulated = modulate(tokens, shift_mod, scale_mod)
    gathered = lax.all_gather(modulated, ("inner", "head"), axis=1, tiled=True)
    clip_count, row_count, model_width = gathered.shape
    flattened = gathered.reshape(clip_count * row_count, model_width)
    local_cols = query_weight.shape[1]
    head_count = local_cols // head_dim
    full_query, full_key, full_value = (
        lax.all_gather(query_weight, "outer", axis=0, tiled=True),
        lax.all_gather(key_weight, "outer", axis=0, tiled=True),
        lax.all_gather(value_weight, "outer", axis=0, tiled=True),
    )
    query_proj = jnp.dot(flattened, full_query, preferred_element_type=jnp.float32)
    key_proj = jnp.dot(flattened, full_key, preferred_element_type=jnp.float32)
    value_proj = jnp.dot(flattened, full_value, preferred_element_type=jnp.float32)
    query_heads = head_norm(
        query_proj.reshape(clip_count, row_count, local_cols), query_gain, head_dim
    )
    key_send = head_norm(key_proj.reshape(clip_count, row_count, local_cols), key_gain, head_dim)
    key_send = key_send.reshape(clip_count, row_count, local_cols)
    value_send = value_proj.astype(jnp.bfloat16).reshape(clip_count, row_count, local_cols)
    root_size = math.sqrt(head_dim)
    full_out = lax.all_gather(out_weight, "outer", axis=1, tiled=True)
    running_max = jnp.full((clip_count, head_count, row_count), -1e30, jnp.float32)
    key_piece = lax.all_gather(key_send, "outer", axis=1, tiled=True)
    value_piece = lax.all_gather(value_send, "outer", axis=1, tiled=True)
    key_count = key_piece.shape[1]
    key_piece = key_piece.reshape(clip_count, key_count, head_count, head_dim)
    value_piece = value_piece.reshape(clip_count, key_count, head_count, head_dim)
    scores = (
        jnp.einsum("cqhd,ckhd->chqk", query_heads, key_piece, preferred_element_type=jnp.float32)
        / root_size
    )
    new_max = jnp.maximum(running_max, jnp.max(scores, axis=-1))
    weights = jnp.exp(scores - new_max[..., None])
    new_sum = jnp.sum(weights, axis=-1)
    new_acc = jnp.einsum(
        "chqk,ckhd->chqd",
        weights.astype(jnp.bfloat16),
        value_piece,
        preferred_element_type=jnp.float32,
    )
    head_out = new_acc / new_sum[..., None]
    mixed = (
        jnp.transpose(head_out, (0, 2, 1, 3))
        .reshape(clip_count * row_count, local_cols)
        .astype(jnp.bfloat16)
    )
    partial_value = jnp.dot(mixed, full_out, preferred_element_type=jnp.float32).reshape(
        clip_count, row_count, -1
    )
    summed = lax.psum_scatter(
        partial_value.astype(jnp.bfloat16), ("inner", "head"), scatter_dimension=1, tiled=True
    ).astype(jnp.float32)
    return (summed * gate_mod[:, None, :]).astype(jnp.bfloat16)


def solution(mesh):
    in_specs = (
        P("clip", ("outer", "inner", "head"), None),
        P("clip", None),
        P("clip", None),
        P("clip", None),
        P("outer", ("inner", "head")),
        P("outer", ("inner", "head")),
        P("outer", ("inner", "head")),
        P(("inner", "head"), "outer"),
        P(),
        P(),
    )
    out_specs = P("clip", ("outer", "inner", "head"), None)
    return jax.shard_map(
        per_device, mesh=mesh, in_specs=in_specs, out_specs=out_specs, check_vma=False
    )
```

profile of v0, /device:TPU:0, one launch (start us, length us, event | category | flops | bytes accessed | tf_op | source)
XLA Modules:
  0.0 723.6 jit_solution(17213850684140932397)
XLA Ops:
  6.5 0.0 copy-start
  6.5 0.0 all-gather.14.cloned.1.call-start
  6.6 0.7 all-gather.14.cloned.1.call-update
  7.3 0.0 all-gather.10.cloned.1.call-start
  7.3 1.7 convert_reduce_fusion
  9.0 0.0 copy-done.2
  9.0 0.6 fusion.12
  9.6 0.0 copy-done.6
  9.6 0.0 copy-done.4
  9.6 1.9 fusion.15
  11.6 0.0 all-gather.10.cloned.1.call-update
  11.6 0.0 all-gather.16.cloned.1.call-start
  11.7 0.7 all-gather.16.cloned.1.call-update
  12.3 0.0 all-gather.12.cloned.1.call-start
  12.4 0.5 all-gather.12.cloned.1.call-update
  12.9 0.0 all-gather.20.cloned.1.call-start
  13.0 0.0 copy-done
  13.0 88.1 %all-gather.14.cloned.1.call-done = bf16[3072,768]{1,0:T(8,128)(2,1)} async-done(((bf16[768,768]{1,0:T(8,128)(2,1)}), bf16[3072,768]{1,0:T(8,128)(2,1)}) %all-gather.14.cloned.1.call-update) | async-done | bytes 4718608 | tf_op jit(solution)/shard_map/all_gather | solution.py:45
  101.1 46.4 %all-gather.10.cloned.1.call-done = bf16[1,1024,3072]{2,1,0:T(8,128)(2,1)} async-done(((bf16[1,256,3072]{2,1,0:T(8,128)(2,1)}), bf16[1,1024,3072]{2,1,0:T(8,128)(2,1)}) %all-gather.10.cloned.1.call-update) | async-done | bytes 6291472 | tf_op jit(solution)/shard_map/all_gather | solution.py:38
  147.4 9.8 %fusion.27 = (f32[1024,768]{0,1:T(8,128)S(1)}, f32[1024,768]{0,1:T(8,128)}) fusion(bf16[3072,768]{1,0:T(8,128)(2,1)} %all-gather.14.cloned.1.call-done, bf16[1,1024,3072]{2,1,0:T(8,128)(2,1)} %all-gather.10.cloned.1.call-done), kind=kOutput, calls=%fused_computation.38 | convolution fusion | flops 4832624640 | bytes 17301504 | tf_op jit(solution)/shard_map/dot_general | solution.py:49
  157.2 0.3 reduce_sum.48
  157.5 3.6 fusion.17
  161.1 0.0 all-gather.20.cloned.1.call-update
  161.2 0.0 all-gather.22.cloned.1.call-start
  161.2 77.2 %all-gather.16.cloned.1.call-done = bf16[3072,768]{1,0:T(8,128)(2,1)} async-done(((bf16[768,768]{1,0:T(8,128)(2,1)}), bf16[3072,768]{1,0:T(8,128)(2,1)}) %all-gather.16.cloned.1.call-update) | async-done | bytes 4718608 | tf_op jit(solution)/shard_map/all_gather | solution.py:46
  238.4 9.4 %fusion.20 = bf16[1024,768]{1,0:T(8,128)(2,1)} fusion(bf16[3072,768]{1,0:T(8,128)(2,1)} %all-gather.16.cloned.1.call-done, bf16[1,1024,3072]{2,1,0:T(8,128)(2,1)} %all-gather.10.cloned.1.call-done), kind=kOutput, calls=%fused_computation.26 | convolution fusion | flops 4832624640 | bytes 12582912 | tf_op jit(solution)/shard_map/dot_general | solution.py:50
  247.8 0.0 all-gather.22.cloned.1.call-update
  247.8 0.0 all-gather.18.cloned.1.call-start
  247.9 0.7 all-gather.18.cloned.1.call-update
  248.6 0.2 reduce-scatter.2.cloned.1.call-start
  248.8 78.9 %all-gather.12.cloned.1.call-done = bf16[3072,768]{1,0:T(8,128)(2,1)} async-done(((bf16[768,768]{1,0:T(8,128)(2,1)}), bf16[3072,768]{1,0:T(8,128)(2,1)}) %all-gather.12.cloned.1.call-update) | async-done | bytes 4718608 | tf_op jit(solution)/shard_map/all_gather | solution.py:44
  327.7 10.3 %fusion.28 = (f32[1024,768]{0,1:T(8,128)}, f32[1024,768]{0,1:T(8,128)}) fusion(bf16[3072,768]{1,0:T(8,128)(2,1)} %all-gather.12.cloned.1.call-done, bf16[1,1024,3072]{2,1,0:T(8,128)(2,1)} %all-gather.10.cloned.1.call-done), kind=kOutput, calls=%fused_computation.39 | convolution fusion | flops 4832624640 | bytes 17301504 | tf_op jit(solution)/shard_map/dot_general | solution.py:48
  338.0 2.6 copy.14
  340.6 0.0 copy-start.3
  340.6 2.2 reduce_sum.47
  342.9 100.0 %all-gather.20.cloned.1.call-done = bf16[4096,768]{0,1:T(8,128)(2,1)} async-done(((bf16[1024,768]{0,1:T(8,128)(2,1)}), bf16[4096,768]{0,1:T(8,128)(2,1)}) %all-gather.20.cloned.1.call-update) | async-done | bytes 6291472 | tf_op jit(solution)/shard_map/all_gather | solution.py:60
  442.9 39.0 %multiply_reduce_fusion = (f32[6,1024]{1,0:T(8,128)S(1)}, f32[6,1024,4096]{2,1,0:T(8,128)}) fusion(bf16[4096,6,128]{0,2,1:T(8,128)(2,1)} %bitcast.44, f32[1024,6,128]{2,0,1:T(8,128)S(1)} %copy.14, f32[128]{0:T(128)S(1)} %copy-done.3, f32[1024,6]{0,1:T(8,128)S(1)} %add_sqrt_fusion.1), kind=kOutput, calls=%fused_computation.1 | convolution fusion | flops 6495135744 | bytes 110150144 | tf_op jit(solution)/shard_map/cqhd,ckhd->chqk/dot_general | solution.py:66
  481.9 76.0 %all-gather.22.cloned.1.call-done = bf16[4096,768]{1,0:T(8,128)(2,1)} async-done(((bf16[1024,768]{1,0:T(8,128)(2,1)}), bf16[4096,768]{1,0:T(8,128)(2,1)}) %all-gather.22.cloned.1.call-update) | async-done | bytes 6291472 | tf_op jit(solution)/shard_map/all_gather | solution.py:61
  557.9 8.8 %copy.16 = bf16[4096,768]{0,1:T(8,128)(2,1)} copy(bf16[4096,768]{1,0:T(8,128)(2,1)} %all-gather.22.cloned.1.call-done) | data formatting | bytes 12582912 | tf_op jit(solution)/shard_map/all_gather | solution.py:61
  566.6 31.5 %fusion = f32[6,1024]{1,0:T(8,128)S(1)} fusion(f32[6,1024,4096]{2,1,0:T(8,128)} %get-tuple-element.10, f32[6,1024]{1,0:T(8,128)S(1)} %broadcast_maximum_fusion), kind=kLoop, calls=%fused_computation.2 | loop fusion | flops 75491328 | bytes 100712448 | tf_op jit(solution)/shard_map/reduce_sum | solution.py:71
  598.1 35.6 %divide_convert_fusion = bf16[6,1024,128]{1,2,0:T(8,128)(2,1)S(1)} fusion(bf16[4096,6,128]{0,2,1:T(8,128)(2,1)} %bitcast.43, f32[6,1024,4096]{2,1,0:T(8,128)} %get-tuple-element.10, f32[6,1024]{1,0:T(8,128)S(1)} %broadcast_maximum_fusion, f32[6,1024]{1,0:T(8,128)S(1)} %fusion), kind=kOutput, calls=%fused_computation.24 | convolution fusion | flops 6519521280 | bytes 108576768 | tf_op jit(solution)/shard_map/chqk,ckhd->chqd/dot_general | solution.py:72
  633.7 13.3 %all-gather.18.cloned.1.call-done = bf16[768,3072]{1,0:T(8,128)(2,1)} async-done(((bf16[768,768]{1,0:T(8,128)(2,1)}), bf16[768,3072]{1,0:T(8,128)(2,1)}) %all-gather.18.cloned.1.call-update) | async-done | bytes 4718608 | tf_op jit(solution)/shard_map/all_gather | solution.py:58
  647.0 9.4 %convert_bitcast_fusion = bf16[1,1024,3072]{2,1,0:T(8,128)(2,1)} fusion(bf16[1024,768]{0,1:T(8,128)(2,1)S(1)} %bitcast.51, bf16[768,3072]{1,0:T(8,128)(2,1)} %all-gather.18.cloned.1.call-done), kind=kOutput, calls=%fused_computation.11 | convolution fusion | flops 4834983936 | bytes 12582912 | tf_op jit(solution)/shard_map/dot_general | solution.py:84
  656.4 0.0 reduce-scatter.2.cloned.1.call-update
  656.4 0.0 copy-start.1
  656.5 57.4 %reduce-scatter.2.cloned.1.call-done = bf16[1,256,3072]{2,1,0:T(8,128)(2,1)} async-done(((bf16[1,1024,3072]{2,1,0:T(8,128)(2,1)}), bf16[1,256,3072]{2,1,0:T(8,128)(2,1)}) %reduce-scatter.2.cloned.1.call-update) | async-done | bytes 1572880 | tf_op jit(solution)/shard_map/reduce_scatter | solution.py:87
  713.8 0.0 copy-done.5
  713.8 2.9 multiply_convert_fusion
  (13 shorter events, 0.1 us)
Async XLA Ops:
  6.5 6.4 copy-start
  6.5 2.5 copy-start.2
  6.5 3.1 copy-start.6
  6.5 3.1 copy-start.4
  6.5 94.5 %all-gather.14.cloned.1.call-start = ((), (), s32[]{:S(2)}) async-start(), calls=%async_computation.3 | async-start | bytes 5898240 | tf_op jit(solution)/shard_map/all_gather | solution.py:45
  7.3 140.1 %all-gather.10.cloned.1.call-start = ((), (), s32[]{:S(2)}) async-start(), calls=%async_computation.1 | async-start | bytes 7864320 | tf_op jit(solution)/shard_map/all_gather | solution.py:38
  11.6 226.8 %all-gather.16.cloned.1.call-start = ((), (), s32[]{:S(2)}) async-start(), calls=%async_computation.4 | async-start | bytes 5898240 | tf_op jit(solution)/shard_map/all_gather | solution.py:46
  12.3 315.3 %all-gather.12.cloned.1.call-start = ((), (), s32[]{:S(2)}) async-start(), calls=%async_computation.2 | async-start | bytes 5898240 | tf_op jit(solution)/shard_map/all_gather | solution.py:44
  12.9 430.0 %all-gather.20.cloned.1.call-start = ((), (), s32[]{:S(2)}) async-start(), calls=%async_computation.7 | async-start | bytes 7864320 | tf_op jit(solution)/shard_map/all_gather | solution.py:60
  161.2 396.7 %all-gather.22.cloned.1.call-start = ((), (), s32[]{:S(2)}) async-start(), calls=%async_computation.8 | async-start | bytes 7864320 | tf_op jit(solution)/shard_map/all_gather | solution.py:61
  247.8 399.2 %all-gather.18.cloned.1.call-start = ((), (), s32[]{:S(2)}) async-start(), calls=%async_computation.5 | async-start | bytes 5898240 | tf_op jit(solution)/shard_map/all_gather | solution.py:58
  248.6 465.3 %reduce-scatter.2.cloned.1.call-start = ((), (), s32[]{:S(2)}) async-start(), calls=%async_computation.6 | async-start | bytes 7864320 | tf_op jit(solution)/shard_map/reduce_scatter | solution.py:87
  340.6 102.2 %copy-start.3 = (f32[128]{0:T(128)S(1)}, f32[128]{0:T(128)}, u32[]{:S(2)}) copy-start(f32[128]{0:T(128)} %param.18) | copy-start | bytes 1540
  656.4 57.4 %copy-start.5 = (f32[1,3072]{1,0:T(1,128)S(1)}, f32[1,3072]{1,0:T(1,128)}, u32[]{:S(2)}) copy-start(f32[1,3072]{1,0:T(1,128)} %param.13) | copy-start | bytes 36868
  656.4 60.3 %copy-start.1 = (f32[128]{0:T(128)S(1)}, f32[128]{0:T(128)}, u32[]{:S(2)}) copy-start(f32[128]{0:T(128)} %param.19) | copy-start | bytes 1540
Sparse Core Ops, SparseCore 0:
  8.9 92.0 all-gather.13
  102.6 44.7 all-gather.9
  149.0 89.3 all-gather.15
  239.8 87.7 all-gather.11
  329.1 113.7 all-gather.19
  444.3 113.5 all-gather.21
  559.4 87.5 all-gather.17
  656.6 57.2 reduce-scatter.1
where the time goes:
time: 724 us
  waiting for transfers between devices  540 us (75%)
  matrix products  113 us (16%)
  other arithmetic  44.7 us (6%)
  between operations  13.6 us (2%)
  local copies, waits for them, and re-layouts  11.4 us (2%)
    all_gather x1, waiting for transfers between devices, per_device(): key_piece = lax.all_gather(key_send, 'outer', axis=1, tiled=True)  100 us
    all_gather x1, waiting for transfers between devices, per_device(): lax.all_gather(key_weight, 'outer', axis=0, tiled=True)  88.1 us
    all_gather x1, waiting for transfers between devices, per_device(): lax.all_gather(query_weight, 'outer', axis=0, tiled=True)  78.9 us
    all_gather x1, waiting for transfers between devices, per_device(): lax.all_gather(value_weight, 'outer', axis=0, tiled=True)  77.2 us
    all_gather x1, waiting for transfers between devices, per_device(): value_piece = lax.all_gather(value_send, 'outer', axis=1, tiled=True)  76 us
    reduce_scatter x1, waiting for transfers between devices, per_device(): lax.psum_scatter(partial_value.astype(jnp.bfloat16), ('inner', 'head'), s...  57.4 us
    all_gather x1, waiting for transfers between devices, per_device(): gathered = lax.all_gather(modulated, ('inner', 'head'), axis=1, tiled=True)  46.4 us
    dot_general x1, matrix products, per_device(): jnp.einsum('cqhd,ckhd->chqk', query_heads, key_piece, preferred_element_t...  39 us
  transfers between devices with their start and end apart: 8, of which 8 were waited for; matrix products, arithmetic and copies ran while one was open for 22% of the time, Pallas kernels for 0%

commit v1 on v0

--- a/solution.py
+++ b/solution.py
@@ -58,7 +58,14 @@
     full_out = lax.all_gather(out_weight, "outer", axis=1, tiled=True)
     running_max = jnp.full((clip_count, head_count, row_count), -1e30, jnp.float32)
     key_piece = lax.all_gather(key_send, "outer", axis=1, tiled=True)
-    value_piece = lax.all_gather(value_send, "outer", axis=1, tiled=True)
+    ring = [value_send]
+    for hop in range(3):
+        ring.append(lax.ppermute(ring[-1], "outer", [(dev, (dev + 1) % 4) for dev in range(4)]))
+    value_piece = jnp.roll(
+        jnp.concatenate(ring[::-1], axis=1),
+        (lax.axis_index("outer") + 1) * ring[0].shape[1],
+        axis=1,
+    )
     key_count = key_piece.shape[1]
     key_piece = key_piece.reshape(clip_count, key_count, head_count, head_dim)
     value_piece = value_piece.reshape(clip_count, key_count, head_count, head_dim)

time: 724 us -> 725 us (level)
  waiting for transfers between devices: 540 us -> 491 us
  starting transfers between devices: 0.49 us -> 39 us
  local copies, waits for them, and re-layouts: 11.4 us -> 22 us
    ppermute x0 -> x3, waiting for transfers between devices: none -> 181 us  [per_device(): lax.ppermute(ring[-1], 'outer', [(dev, (dev + 1) % 4) for dev in range(4)])]
    all_gather x1, waiting for transfers between devices: 78.9 us -> 0.01 us  [per_device(): lax.all_gather(query_weight, 'outer', axis=0, tiled=True)]
    all_gather x1 -> x0, waiting for transfers between devices: 76 us -> none  [per_device(): value_piece = lax.all_gather(value_send, 'outer', axis=1, tiled=True)]
    all_gather x1, waiting for transfers between devices: 100 us -> 28.3 us  [per_device(): key_piece = lax.all_gather(key_send, 'outer', axis=1, tiled=True)]
    ppermute x0 -> x3, starting transfers between devices: none -> 38.7 us  [per_device(): lax.ppermute(ring[-1], 'outer', [(dev, (dev + 1) % 4) for dev in range(4)])]
    all_gather x1, waiting for transfers between devices: 13.3 us -> 0.02 us  [per_device(): full_out = lax.all_gather(out_weight, 'outer', axis=1, tiled=True)]
    reduce_scatter x1, waiting for transfers between devices: 57.4 us -> 70 us  [per_device(): lax.psum_scatter(partial_value.astype(jnp.bfloat16), ('inner', 'head'), s...]
    dynamic_slice x0 -> x2, local copies, waits for them, and re-layouts: none -> 11.9 us  [per_device(): jnp.roll(jnp.concatenate(ring[::-1], axis=1), (lax.axis_index('outer') +...]
  transfers between devices with their start and end apart: 8 -> 10, of which waited for: 8 -> 8; matrix products, arithmetic and copies ran while one was open for 22% -> 23% of each run, Pallas kernels for 0% -> 0%
where the time goes in v1:
time: 725 us
  waiting for transfers between devices  491 us (68%)
  matrix products  112 us (15%)
  other arithmetic  47.3 us (7%)
  starting transfers between devices  39 us (5%)
  local copies, waits for them, and re-layouts  22 us (3%)
  between operations  13.7 us (2%)
    ppermute x3, waiting for transfers between devices, per_device(): lax.ppermute(ring[-1], 'outer', [(dev, (dev + 1) % 4) for dev in range(4)])  181 us
    all_gather x1, waiting for transfers between devices, per_device(): lax.all_gather(key_weight, 'outer', axis=0, tiled=True)  85.3 us
    all_gather x1, waiting for transfers between devices, per_device(): lax.all_gather(value_weight, 'outer', axis=0, tiled=True)  77.2 us
    reduce_scatter x1, waiting for transfers between devices, per_device(): lax.psum_scatter(partial_value.astype(jnp.bfloat16), ('inner', 'head'), s...  70 us
    all_gather x1, waiting for transfers between devices, per_device(): gathered = lax.all_gather(modulated, ('inner', 'head'), axis=1, tiled=True)  46.4 us
    ppermute x3, starting transfers between devices, per_device(): lax.ppermute(ring[-1], 'outer', [(dev, (dev + 1) % 4) for dev in range(4)])  38.7 us
    dot_general x1, matrix products, per_device(): jnp.einsum('cqhd,ckhd->chqk', query_heads, key_piece, preferred_element_t...  38.6 us
    dot_general x1, matrix products, per_device(): jnp.einsum('chqk,ckhd->chqd', weights.astype(jnp.bfloat16), value_piece,...  35.5 us
  transfers between devices with their start and end apart: 10, of which 8 were waited for; matrix products, arithmetic and copies ran while one was open for 23% of the time, Pallas kernels for 0%

profile of v1, /device:TPU:0, one launch (start us, length us, event | category | flops | bytes accessed | tf_op | source)
XLA Modules:
  0.0 724.7 jit_solution(4443547460985664975)
XLA Ops:
  6.5 0.7 all-gather.12.cloned.1.call-update
  7.3 0.0 all-gather.8.cloned.1.call-start
  7.3 1.7 convert_reduce_fusion
  9.0 2.0 fusion.12
  11.0 0.7 broadcast_add_fusion
  11.7 2.6 fusion.15
  14.4 0.0 all-gather.8.cloned.1.call-update
  14.4 0.0 all-gather.14.cloned.1.call-start
  14.4 0.7 all-gather.14.cloned.1.call-update
  15.1 0.0 all-gather.10.cloned.1.call-start
  15.2 0.5 all-gather.10.cloned.1.call-update
  15.7 0.0 all-gather.18.cloned.1.call-start
  15.8 85.3 %all-gather.12.cloned.1.call-done = bf16[3072,768]{1,0:T(8,128)(2,1)} async-done(((bf16[768,768]{1,0:T(8,128)(2,1)}), bf16[3072,768]{1,0:T(8,128)(2,1)}) %all-gather.12.cloned.1.call-update) | async-done | bytes 4718608 | tf_op jit(solution)/shard_map/all_gather | solution.py:45
  101.0 46.4 %all-gather.8.cloned.1.call-done = bf16[1,1024,3072]{2,1,0:T(8,128)(2,1)} async-done(((bf16[1,256,3072]{2,1,0:T(8,128)(2,1)}), bf16[1,1024,3072]{2,1,0:T(8,128)(2,1)}) %all-gather.8.cloned.1.call-update) | async-done | bytes 6291472 | tf_op jit(solution)/shard_map/all_gather | solution.py:38
  147.4 9.8 %fusion.30 = (f32[1024,768]{0,1:T(8,128)S(1)}, f32[1024,768]{0,1:T(8,128)}) fusion(bf16[3072,768]{1,0:T(8,128)(2,1)} %all-gather.12.cloned.1.call-done, bf16[1,1024,3072]{2,1,0:T(8,128)(2,1)} %all-gather.8.cloned.1.call-done), kind=kOutput, calls=%fused_computation.48 | convolution fusion | flops 4832624640 | bytes 17301504 | tf_op jit(solution)/shard_map/dot_general | solution.py:49
  157.2 0.3 reduce_sum.48
  157.5 3.6 fusion.17
  161.1 0.0 all-gather.16.cloned.1.call-start
  161.2 77.2 %all-gather.14.cloned.1.call-done = bf16[3072,768]{1,0:T(8,128)(2,1)} async-done(((bf16[768,768]{1,0:T(8,128)(2,1)}), bf16[3072,768]{1,0:T(8,128)(2,1)}) %all-gather.14.cloned.1.call-update) | async-done | bytes 4718608 | tf_op jit(solution)/shard_map/all_gather | solution.py:46
  238.4 8.5 %fusion.26 = bf16[1,1024,768]{2,1,0:T(8,128)(2,1)S(1)} fusion(bf16[3072,768]{1,0:T(8,128)(2,1)} %all-gather.14.cloned.1.call-done, bf16[1,1024,3072]{2,1,0:T(8,128)(2,1)} %all-gather.8.cloned.1.call-done), kind=kOutput, calls=%fused_computation.30 | convolution fusion | flops 4832624640 | bytes 12582912 | tf_op jit(solution)/shard_map/dot_general | solution.py:50
  246.9 1.1 copy-done.3
  248.1 72.3 %collective-permute-done = bf16[1,1024,768]{2,1,0:T(8,128)(2,1)S(1)} collective-permute-done((bf16[1,1024,768]{2,1,0:T(8,128)(2,1)S(1)}, bf16[1,1024,768]{2,1,0:T(8,128)(2,1)S(1)}, u32[]{:S(2)}, u32[]{:S(2)}) %collective-permute-start) | collective-permute-done | bytes 1572896 | tf_op jit(solution)/shard_map/ppermute | solution.py:63
  320.4 30.5 %collective-permute-start.1 = (bf16[1,1024,768]{2,1,0:T(8,128)(2,1)S(1)}, bf16[1,1024,768]{2,1,0:T(8,128)(2,1)}, u32[]{:S(2)}, u32[]{:S(2)}) collective-permute-start(bf16[1,1024,768]{2,1,0:T(8,128)(2,1)S(1)} %collective-permute-done), channel_id=1, source_target_pairs={{0,4},{4,8},{8,12},{12,0},{1,5},{5,9},{9,13},{13,1},{2,6},{6,10},{... | collective-permute-start | bytes 4718600 | tf_op jit(solution)/shard_map/ppermute | solution.py:63
  350.9 0.0 reduce-scatter.2.cloned.1.call-start
  351.0 55.7 %collective-permute-done.1 = bf16[1,1024,768]{2,1,0:T(8,128)(2,1)} collective-permute-done((bf16[1,1024,768]{2,1,0:T(8,128)(2,1)S(1)}, bf16[1,1024,768]{2,1,0:T(8,128)(2,1)}, u32[]{:S(2)}, u32[]{:S(2)}) %collective-permute-start.1) | collective-permute-done | bytes 1572896 | tf_op jit(solution)/shard_map/ppermute | solution.py:63
  406.7 8.3 %collective-permute-start.2 = (bf16[1,1024,768]{2,1,0:T(8,128)(2,1)}, bf16[1,1024,768]{2,1,0:T(8,128)(2,1)}, u32[]{:S(2)}, u32[]{:S(2)}) collective-permute-start(bf16[1,1024,768]{2,1,0:T(8,128)(2,1)} %collective-permute-done.1), channel_id=1, source_target_pairs={{0,4},{4,8},{8,12},{12,0},{1,5},{5,9},{9,13},{13,1},{2,6},{6,10},{... | collective-permute-start | bytes 4718600 | tf_op jit(solution)/shard_map/ppermute | solution.py:63
  414.9 10.3 %fusion.31 = (f32[1024,768]{0,1:T(8,128)}, f32[1024,768]{0,1:T(8,128)}) fusion(bf16[3072,768]{1,0:T(8,128)(2,1)} %all-gather.10.cloned.1.call-done, bf16[1,1024,3072]{2,1,0:T(8,128)(2,1)} %all-gather.8.cloned.1.call-done), kind=kOutput, calls=%fused_computation.49 | convolution fusion | flops 4832624640 | bytes 17301504 | tf_op jit(solution)/shard_map/dot_general | solution.py:48
  425.2 2.4 copy.13
  427.6 2.2 reduce_sum.47
  429.9 53.5 %collective-permute-done.2 = bf16[1,1024,768]{2,1,0:T(8,128)(2,1)} collective-permute-done((bf16[1,1024,768]{2,1,0:T(8,128)(2,1)}, bf16[1,1024,768]{2,1,0:T(8,128)(2,1)}, u32[]{:S(2)}, u32[]{:S(2)}) %collective-permute-start.2) | collective-permute-done | bytes 1572896 | tf_op jit(solution)/shard_map/ppermute | solution.py:63
  483.4 1.5 constant_dynamic-update-slice_fusion.7
  484.9 1.5 constant_dynamic-update-slice_fusion.6
  486.4 0.1 constant_dynamic-update-slice_fusion.5
  486.5 0.1 constant_dynamic-update-slice_fusion.4
  486.7 1.5 constant_dynamic-update-slice_fusion.3
  488.2 1.5 constant_dynamic-update-slice_fusion.2
  489.7 0.1 constant_dynamic-update-slice_fusion.1
  489.8 0.1 constant_dynamic-update-slice_fusion
  489.9 3.1 constant_dynamic-slice_fusion
  493.0 8.8 %copy.15 = bf16[1,4096,768]{1,2,0:T(8,128)(2,1)} copy(bf16[1,4096,768]{2,1,0:T(8,128)(2,1)} %constant_dynamic-slice_fusion) | data formatting | bytes 12582912 | tf_op jit(solution)/shard_map/jit(_roll_dynamic)/dynamic_slice | solution.py:64
  501.8 28.3 %all-gather.18.cloned.1.call-done = bf16[4096,768]{0,1:T(8,128)(2,1)} async-done(((bf16[1024,768]{0,1:T(8,128)(2,1)}), bf16[4096,768]{0,1:T(8,128)(2,1)}) %all-gather.18.cloned.1.call-update) | async-done | bytes 6291472 | tf_op jit(solution)/shard_map/all_gather | solution.py:60
  530.1 38.6 %multiply_reduce_fusion = (f32[6,1024]{1,0:T(8,128)S(1)}, f32[6,1024,4096]{2,1,0:T(8,128)}) fusion(bf16[4096,6,128]{0,2,1:T(8,128)(2,1)} %bitcast.48, f32[1024,6,128]{2,0,1:T(8,128)S(1)} %copy.13, f32[128]{0:T(128)S(1)} %copy-done.7, f32[1024,6]{0,1:T(8,128)S(1)} %add_sqrt_fusion.1), kind=kOutput, calls=%fused_computation.1 | convolution fusion | flops 6495135744 | bytes 110150144 | tf_op jit(solution)/shard_map/cqhd,ckhd->chqk/dot_general | solution.py:73
  568.8 31.2 %fusion = f32[6,1024]{1,0:T(8,128)S(1)} fusion(f32[6,1024,4096]{2,1,0:T(8,128)} %get-tuple-element.10, f32[6,1024]{1,0:T(8,128)S(1)} %broadcast_maximum_fusion), kind=kLoop, calls=%fused_computation.2 | loop fusion | flops 75491328 | bytes 100712448 | tf_op jit(solution)/shard_map/reduce_sum | solution.py:78
  600.0 35.5 %divide_convert_fusion = bf16[6,1024,128]{1,2,0:T(8,128)(2,1)S(1)} fusion(bf16[4096,6,128]{0,2,1:T(8,128)(2,1)} %bitcast.47, f32[6,1024,4096]{2,1,0:T(8,128)} %get-tuple-element.10, f32[6,1024]{1,0:T(8,128)S(1)} %broadcast_maximum_fusion, f32[6,1024]{1,0:T(8,128)S(1)} %fusion), kind=kOutput, calls=%fused_computation.24 | convolution fusion | flops 6519521280 | bytes 108576768 | tf_op jit(solution)/shard_map/chqk,ckhd->chqd/dot_general | solution.py:79
  635.6 0.0 all-gather.16.cloned.1.call-done
  635.6 9.4 %convert_bitcast_fusion = bf16[1,1024,3072]{2,1,0:T(8,128)(2,1)} fusion(bf16[1024,768]{0,1:T(8,128)(2,1)S(1)} %bitcast.55, bf16[768,3072]{1,0:T(8,128)(2,1)} %all-gather.16.cloned.1.call-done), kind=kOutput, calls=%fused_computation.11 | convolution fusion | flops 4834983936 | bytes 12582912 | tf_op jit(solution)/shard_map/dot_general | solution.py:91
  645.0 70.0 %reduce-scatter.2.cloned.1.call-done = bf16[1,256,3072]{2,1,0:T(8,128)(2,1)} async-done(((bf16[1,1024,3072]{2,1,0:T(8,128)(2,1)}), bf16[1,256,3072]{2,1,0:T(8,128)(2,1)}) %reduce-scatter.2.cloned.1.call-update) | async-done | bytes 1572880 | tf_op jit(solution)/shard_map/reduce_scatter | solution.py:94
  715.0 2.9 multiply_convert_fusion
  (29 shorter events, 0.1 us)
Async XLA Ops:
  6.5 9.2 %copy-start = (f32[128]{0:T(128)S(1)}, f32[128]{0:T(128)}, u32[]{:S(2)}) copy-start(f32[128]{0:T(128)} %param.19) | copy-start | bytes 1540
  6.5 5.2 copy-start.2
  6.5 94.5 %all-gather.12.cloned.1.call-start = ((), (), s32[]{:S(2)}) async-start(), calls=%async_computation.3 | async-start | bytes 5898240 | tf_op jit(solution)/shard_map/all_gather | solution.py:45
  7.3 140.1 %all-gather.8.cloned.1.call-start = ((), (), s32[]{:S(2)}) async-start(), calls=%async_computation.1 | async-start | bytes 7864320 | tf_op jit(solution)/shard_map/all_gather | solution.py:38
  14.4 224.0 %all-gather.14.cloned.1.call-start = ((), (), s32[]{:S(2)}) async-start(), calls=%async_computation.4 | async-start | bytes 5898240 | tf_op jit(solution)/shard_map/all_gather | solution.py:46
  15.1 399.8 %all-gather.10.cloned.1.call-start = ((), (), s32[]{:S(2)}) async-start(), calls=%async_computation.2 | async-start | bytes 5898240 | tf_op jit(solution)/shard_map/all_gather | solution.py:44
  15.7 514.4 %all-gather.18.cloned.1.call-start = ((), (), s32[]{:S(2)}) async-start(), calls=%async_computation.7 | async-start | bytes 7864320 | tf_op jit(solution)/shard_map/all_gather | solution.py:60
  161.1 474.4 %all-gather.16.cloned.1.call-start = ((), (), s32[]{:S(2)}) async-start(), calls=%async_computation.5 | async-start | bytes 5898240 | tf_op jit(solution)/shard_map/all_gather | solution.py:58
  246.9 1.1 copy-start.3
  248.1 72.3 %collective-permute-start = (bf16[1,1024,768]{2,1,0:T(8,128)(2,1)S(1)}, bf16[1,1024,768]{2,1,0:T(8,128)(2,1)S(1)}, u32[]{:S(2)}, u32[]{:S(2)}) collective-permute-start(bf16[1,1024,768]{2,1,0:T(8,128)(2,1)S(1)} %fusion.26), channel_id=1, source_target_pairs={{0,4},{4,8},{8,12},{12,0},{1,5},{5,9},{9,13},{13,1},{2,6},{6,10},{... | collective-permute-start | bytes 4718600 | tf_op jit(solution)/shard_map/ppermute | solution.py:63
  320.4 104.8 %copy-start.5 = (bf16[1,1024,768]{2,1,0:T(8,128)(2,1)}, bf16[1,1024,768]{2,1,0:T(8,128)(2,1)S(1)}, u32[]{:S(2)}) copy-start(bf16[1,1024,768]{2,1,0:T(8,128)(2,1)S(1)} %collective-permute-done) | copy-start | bytes 4718596
  320.4 86.2 %collective-permute-start.1 = (bf16[1,1024,768]{2,1,0:T(8,128)(2,1)S(1)}, bf16[1,1024,768]{2,1,0:T(8,128)(2,1)}, u32[]{:S(2)}, u32[]{:S(2)}) collective-permute-start(bf16[1,1024,768]{2,1,0:T(8,128)(2,1)S(1)} %collective-permute-done), channel_id=1, source_target_pairs={{0,4},{4,8},{8,12},{12,0},{1,5},{5,9},{9,13},{13,1},{2,6},{6,10},{... | collective-permute-start | bytes 4718600 | tf_op jit(solution)/shard_map/ppermute | solution.py:63
  350.9 364.1 %reduce-scatter.2.cloned.1.call-start = ((), (), s32[]{:S(2)}) async-start(), calls=%async_computation.6 | async-start | bytes 7864320 | tf_op jit(solution)/shard_map/reduce_scatter | solution.py:94
  406.7 76.7 %collective-permute-start.2 = (bf16[1,1024,768]{2,1,0:T(8,128)(2,1)}, bf16[1,1024,768]{2,1,0:T(8,128)(2,1)}, u32[]{:S(2)}, u32[]{:S(2)}) collective-permute-start(bf16[1,1024,768]{2,1,0:T(8,128)(2,1)} %collective-permute-done.1), channel_id=1, source_target_pairs={{0,4},{4,8},{8,12},{12,0},{1,5},{5,9},{9,13},{13,1},{2,6},{6,10},{... | collective-permute-start | bytes 4718600 | tf_op jit(solution)/shard_map/ppermute | solution.py:63
  429.8 56.6 %copy-start.6 = (bf16[1,1024,768]{2,1,0:T(8,128)(2,1)S(1)}, bf16[1,1024,768]{2,1,0:T(8,128)(2,1)}, u32[]{:S(2)}) copy-start(bf16[1,1024,768]{2,1,0:T(8,128)(2,1)} %copy-done.5) | copy-start | bytes 4718596
  429.9 56.7 %copy-start.4 = (bf16[1,1024,768]{2,1,0:T(8,128)(2,1)S(1)}, bf16[1,1024,768]{2,1,0:T(8,128)(2,1)}, u32[]{:S(2)}) copy-start(bf16[1,1024,768]{2,1,0:T(8,128)(2,1)} %copy-done.3) | copy-start | bytes 4718596
  493.0 37.1 %copy-start.7 = (f32[128]{0:T(128)S(1)}, f32[128]{0:T(128)}, u32[]{:S(2)}) copy-start(f32[128]{0:T(128)} %param.18) | copy-start | bytes 1540
  645.0 70.0 %copy-start.8 = (f32[1,3072]{1,0:T(1,128)S(1)}, f32[1,3072]{1,0:T(1,128)}, u32[]{:S(2)}) copy-start(f32[1,3072]{1,0:T(1,128)} %param.13) | copy-start | bytes 36868
  645.0 72.9 %copy-start.1 = (f32[128]{0:T(128)S(1)}, f32[128]{0:T(128)}, u32[]{:S(2)}) copy-start(f32[128]{0:T(128)} %param.19) | copy-start | bytes 1540
Sparse Core Ops, SparseCore 0:
  8.9 92.1 all-gather.11
  102.6 44.7 all-gather.7
  149.0 89.3 all-gather.13
  239.8 130.4 all-gather.9
  371.8 158.2 all-gather.17
  531.5 87.5 all-gather.15
  645.1 69.8 reduce-scatter.1
